TPU v7x, 128 devices: a whole 4x4x4 slice. The times are simulated.
128 devices in a mesh: gene: 8 (over x, core), site: 16 (over z, y).
Axes of the slice: x: 4, y: 4, z: 4, core: 2. Of those that a mesh axis runs over, the one named last changes fastest.
Arguments:
- tips: bfloat16 [8, 32, 20, 32768], P('gene', None, None, 'site'), may hold values from 0.0009994507 to 1
- exchange: float32 [20, 20], replicated, may hold values from 0.05 to 5
- freqs: float32 [20], replicated, may hold values from 0.02 to 0.12
- rates: float32 [4], replicated, may hold values from 0.1 to 3
- branch: float32 [62], replicated, may hold values from 0.02 to 0.6
- children: int32 [31, 2], replicated, may hold values from 0 to 61, as said below
- slot_gene: int32 [8, 256], P('gene', 'site'), may hold values from 0 to 63, as said below
- site_count: int32 [8, 256], P('gene', 'site'), may hold values from 0 to 128, as said below
Outputs:
- site_loglik: float32 [8, 32768], P('gene', 'site')
- gene_loglik: float32 [8, 64], P('gene')
- total: float32 [], replicated
Inputs may be any that keep to these rules, and one draw needn't show every extreme that they name: `children`: internal nodes come in 5 levels: the first 16 pair up all leaves, each next level pairs up all nodes of the level before, in node order; each node is a child once. On each device along site the slots with site_count > 0 come first; each device holds at least (64 + 16 - 1) // 16 of them and in each group one device has all 16 live; a live slot's live sites are its first ones. `slot_gene`: every gene of a group owns at least one live slot; on slots that are not live the value is 0.
All inputs are finite; a program needn't handle non-finite values.
Results may differ from a plain program's by a relative error of at most 0.0003.
Values may be sent and summed in bfloat16 or wider, within the bound.
A program may use at most 128 MiB of HBM per device.

v0:
```python
import functools

import jax
import jax.numpy as jnp
from jax import lax
from jax.experimental import pallas as pl
from jax.experimental.pallas import tpu as pltpu
from jax.sharding import PartitionSpec as P

STATES = 20
RATES = 4
ROWS = STATES * RATES
LEAVES = 32
INNER = 30
NODES = 62
GENES = 64
PAD = 24
LANES = 128
SPLIT = 32
BLOCK = 512
F32 = jnp.float32
BF16 = jnp.bfloat16


def iota(shape, axis):
    return lax.broadcasted_iota(jnp.int32, shape, axis)


def rate_powers(exchange_ref, freqs_ref, pad_ref):
    pad_ref[...] = jnp.zeros((LANES, LANES), F32)
    pad_ref[0:STATES, 0:STATES] = exchange_ref[...]
    full = pad_ref[...]
    both = (full + full.T)[0:PAD, :]
    shape = (PAD, LANES)
    sub, lane = iota(shape, 0), iota(shape, 1)
    pi_sub = jnp.zeros(shape, F32)
    pi_lane = jnp.zeros(shape, F32)
    for state in range(STATES):
        value = freqs_ref[state]
        pi_sub = jnp.where(sub == state, value, pi_sub)
        pi_lane = jnp.where(lane == state, value, pi_lane)
    total = jnp.sum(pi_sub, axis=0, keepdims=True)
    pi_sub = pi_sub / total
    pi_lane = pi_lane / total
    off = jnp.where(sub == lane, 0.0, both * 0.5 * pi_sub)
    out_rate = jnp.sum(off, axis=0, keepdims=True)
    mean_rate = jnp.sum(out_rate * pi_lane[0:1], axis=1, keepdims=True)
    gen = (off - jnp.where(sub == lane, out_rate, 0.0)) / mean_rate

    def times(left, right):
        acc = left[:, 0:1] * right[0:1, :]
        for mid in range(1, STATES):
            acc = acc + left[:, mid : mid + 1] * right[mid : mid + 1, :]
        return acc

    second = times(gen, gen) * 0.5
    third = times(second, gen) * (1.0 / 3.0)
    fourth = times(second, second) * (4.0 / 24.0)
    powers = [gen, second, third, fourth]
    for order, part in ((5, gen), (6, second), (7, third), (8, fourth)):
        ratio = {5: 24.0 / 120.0, 6: 48.0 / 720.0, 7: 144.0 / 5040.0, 8: 576.0 / 40320.0}[order]
        powers.append(times(fourth, part) * ratio)
    return powers, pi_sub


def transitions(powers, rates_ref, branch_ref, mat_ref):
    shape = (1, LANES)
    lane = iota(shape, 1)
    category = lane // SPLIT
    rate = jnp.zeros(shape, F32)
    mean = jnp.zeros(shape, F32)
    for k in range(RATES):
        rate = jnp.where(category == k, rates_ref[k], rate)
        mean = mean + rates_ref[k]
    rate = rate / (mean / RATES)
    taus = []
    for half in range(2):
        length = jnp.zeros(shape, F32)
        for at in range(min(SPLIT, NODES - half * SPLIT)):
            length = jnp.where(lane % SPLIT == at, branch_ref[half * SPLIT + at], length)
        taus.append(length * rate / 256.0)
    sub = iota((PAD, LANES), 0)
    for i in range(STATES):
        columns = [jnp.broadcast_to(p[:, i : i + 1], (PAD, LANES)) for p in powers]
        eye = jnp.where(sub == i, 1.0, 0.0)
        for half in range(2):
            acc = columns[7]
            for order in range(6, -1, -1):
                acc = columns[order] + acc * taus[half]
            mat_ref[0, half, i * PAD : (i + 1) * PAD, :] = eye + acc * taus[half]

    def square(step, carry):
        src = lax.rem(step, 2)
        dst = 1 - src
        for half in range(2):
            for first in range(0, STATES, 4):
                accs = [None] * 4
                for mid in range(STATES):
                    row = mat_ref[src, half, mid * PAD : (mid + 1) * PAD, :]
                    for at in range(4):
                        where = (first + at) * PAD + mid
                        factor = mat_ref[src, half, where : where + 1, :]
                        term = factor * row
                        accs[at] = term if accs[at] is None else accs[at] + term
                for at in range(4):
                    start = (first + at) * PAD
                    mat_ref[dst, half, start : start + PAD, :] = accs[at]
        return carry

    lax.fori_loop(0, 8, square, 0)


def operands(children_ref, mat_ref, spread_ref, leaf_ref, inner_ref):
    for half in range(2):
        for group in range(4):
            block = mat_ref[0, half, group * 120 : group * 120 + LANES, :].T
            for at in range(5):
                i = group * 5 + at
                moved = block if at == 0 else pltpu.roll(block, LANES - PAD * at, 1)
                spread_ref[half, i * LANES : (i + 1) * LANES, :] = moved

    lane = iota((ROWS, LANES), 1)

    def parts(half, at):
        value = spread_ref[half, pl.ds(at, ROWS, stride=SPLIT), :]
        value = jnp.where(lane < STATES, value, 0.0)
        high = value.astype(BF16).astype(F32)
        return high, value - high

    for node in range(LEAVES // 2):
        high, low = parts(0, children_ref[0, node])
        leaf_ref[node, 0:ROWS, :] = (high + pltpu.roll(low, 32, 1)).astype(BF16)
        high, low = parts(0, children_ref[1, node])
        leaf_ref[node, ROWS : 2 * ROWS, :] = (
            pltpu.roll(high, 64, 1) + pltpu.roll(low, 96, 1)
        ).astype(BF16)

    row, col = iota((LANES, 256), 0), iota((LANES, 256), 1)
    state = lax.rem(col, ROWS) // RATES
    low_part = (col >= 2 * ROWS).astype(jnp.int32) * 32
    place = jnp.where((row == state + low_part) & (col < 3 * ROWS), 1.0, 0.0).astype(BF16)
    row, col = iota((ROWS, 256), 0), iota((ROWS, 256), 1)
    same = lax.rem(row, RATES) == lax.rem(col, RATES)
    for at in range(INNER):
        high, low = parts(1, at)
        both = (high + pltpu.roll(low, 32, 1)).astype(BF16)
        wide = jnp.dot(both, place, preferred_element_type=F32)
        inner_ref[at] = jnp.where(same, wide, 0.0).astype(BF16)


def prune_block(start, tips_ref, children_ref, leaf_ref, inner_ref, flat_ref, node_ref, weight):
    tiles = BLOCK // LANES
    for tile in range(tiles):
        lanes = pl.ds(start + tile * LANES, LANES)
        for state in range(STATES):
            rows = slice(state * LEAVES, (state + 1) * LEAVES)
            flat_ref[tile, rows, :] = tips_ref[state, :, lanes].astype(F32)

    def keep(at, value):
        high = value.astype(BF16)
        node_ref[at, 0:ROWS, :] = high
        node_ref[at, ROWS : 2 * ROWS, :] = (value - high.astype(F32)).astype(BF16)

    filler = jnp.zeros((SPLIT - PAD, BLOCK), F32)

    def leaf(at):
        rows = pl.ds(at, PAD, stride=LEAVES)
        value = jnp.concatenate([flat_ref[tile, rows, :] for tile in range(tiles)], axis=1)
        return jnp.concatenate([value, filler], axis=0).astype(BF16)

    for node in range(LEAVES // 2):
        left = leaf(children_ref[0, node])
        right = leaf(children_ref[1, node])
        stacked = jnp.concatenate([left, left, right, right], axis=0)
        both = jnp.dot(leaf_ref[node], stacked, preferred_element_type=F32)
        keep(node, both[0:ROWS] * both[ROWS:])

    def moved(child):
        high = node_ref[child, 0:ROWS, :]
        low = node_ref[child, ROWS : 2 * ROWS, :]
        stacked = jnp.concatenate([high, low, high, high[0:16]], axis=0)
        return jnp.dot(inner_ref[child], stacked, preferred_element_type=F32)

    scale = jnp.zeros((1, BLOCK), F32)
    node = LEAVES // 2
    for count in (8, 4, 2, 1):
        for _ in range(count):
            left = children_ref[0, node] - LEAVES
            right = children_ref[1, node] - LEAVES
            value = moved(left) * moved(right)
            if count == 4:
                top = jnp.max(value, axis=0, keepdims=True)
                value = value * (1.0 / top)
                scale = scale + jnp.log(top)
            if count > 1:
                keep(node, value)
            node = node + 1
    lik = jnp.sum(value * weight, axis=0, keepdims=True)
    return jnp.log(lik) + scale


def local_kernel(
    children_ref,
    gene_ref,
    count_ref,
    freqs_ref,
    rates_ref,
    branch_ref,
    exchange_ref,
    tips_hbm,
    site_ref,
    part_ref,
    tips_ref,
    pad_ref,
    mat_ref,
    spread_ref,
    leaf_ref,
    inner_ref,
    flat_ref,
    node_ref,
    weight_ref,
    sem,
):
    fetch = pltpu.make_async_copy(tips_hbm.at[0], tips_ref, sem)
    fetch.start()
    powers, pi_sub = rate_powers(exchange_ref, freqs_ref, pad_ref)
    for i in range(STATES):
        row = jnp.broadcast_to(pi_sub[i : i + 1, 0:1] / RATES, (RATES, LANES))
        weight_ref[i * RATES : (i + 1) * RATES, :] = row
    transitions(powers, rates_ref, branch_ref, mat_ref)
    operands(children_ref, mat_ref, spread_ref, leaf_ref, inner_ref)
    part_ref[...] = jnp.zeros((1, LANES), F32)
    for tile in range(BLOCK // LANES):
        empty = jnp.zeros(((PAD - STATES) * LEAVES, LANES), F32)
        flat_ref[tile, STATES * LEAVES :, :] = empty
    fetch.wait()

    def step(number, carry):
        start = pl.multiple_of(number * BLOCK, BLOCK)
        weight = weight_ref[:, 0:1]
        values = prune_block(
            start, tips_ref, children_ref, leaf_ref, inner_ref, flat_ref, node_ref, weight
        )
        lane = iota((1, LANES), 1)
        for at in range(BLOCK // LANES):
            slot = number * (BLOCK // LANES) + at
            live = count_ref[0, slot]
            gene = gene_ref[0, slot]
            part = values[:, at * LANES : (at + 1) * LANES]
            part = jnp.where(lane < live, part, 0.0)
            site_ref[:, pl.ds(start + at * LANES, LANES)] = part
            summed = jnp.sum(part, axis=1, keepdims=True)
            add = jnp.where(lane == gene, summed, 0.0)
            add = add + jnp.where(lane == gene + GENES, live.astype(F32), 0.0)
            part_ref[...] = part_ref[...] + add
        return carry

    lax.fori_loop(0, site_ref.shape[1] // BLOCK, step, 0)


def local_part(tips, exchange, freqs, rates, branch, children, slot_gene, site_count):
    sites = tips.shape[3]
    smem = pl.BlockSpec(memory_space=pltpu.SMEM)
    vmem = pl.BlockSpec(memory_space=pltpu.VMEM)
    return pl.pallas_call(
        local_kernel,
        name="local_part",
        out_shape=(
            jax.ShapeDtypeStruct((1, sites), F32),
            jax.ShapeDtypeStruct((1, LANES), F32),
        ),
        in_specs=[smem] * 6 + [vmem, pl.BlockSpec(memory_space=pl.ANY)],
        out_specs=(vmem, vmem),
        scratch_shapes=[
            pltpu.VMEM((STATES, LEAVES, sites), BF16),
            pltpu.VMEM((LANES, LANES), F32),
            pltpu.VMEM((2, 2, 512, LANES), F32),
            pltpu.VMEM((2, STATES * LANES, LANES), F32),
            pltpu.VMEM((LEAVES // 2, 2 * ROWS, LANES), BF16),
            pltpu.VMEM((INNER, ROWS, 256), BF16),
            pltpu.VMEM((BLOCK // LANES, PAD * LEAVES, LANES), F32),
            pltpu.VMEM((INNER, 2 * ROWS, BLOCK), BF16),
            pltpu.VMEM((ROWS, LANES), F32),
            pltpu.SemaphoreType.DMA,
        ],
        compiler_params=pltpu.CompilerParams(vmem_limit_bytes=60 * 1024 * 1024),
    )(children.T, slot_gene, site_count, freqs, rates, branch, exchange, tips.transpose(0, 2, 1, 3))


def sum_kernel(genes, sites, scale, part_ref, gene_ref, total_ref, site_buf, gene_buf, own_ref, site_send, site_recv, gene_send, gene_recv):
    group = lax.axis_index("gene")
    member = lax.axis_index("site")
    barrier = pltpu.get_barrier_semaphore()
    for off in range(1, sites):
        pl.semaphore_signal(barrier, inc=1, device_id={"site": lax.rem(member + off, sites)})
    for off in range(1, genes):
        pl.semaphore_signal(barrier, inc=1, device_id={"gene": lax.rem(group + off, genes)})
    pl.semaphore_wait(barrier, sites + genes - 2)
    copies = []
    for off in range(1, sites):
        copies.append(
            pltpu.make_async_remote_copy(
                src_ref=part_ref,
                dst_ref=site_buf.at[member],
                send_sem=site_send.at[off],
                recv_sem=site_recv.at[off],
                device_id={"site": lax.rem(member + off, sites)},
            )
        )
    for copy in copies:
        copy.start()
    site_buf[member] = part_ref[...]
    for copy in copies:
        copy.wait()
    summed = site_buf[0]
    for at in range(1, sites):
        summed = summed + site_buf[at]
    counts = pltpu.roll(summed, GENES, 1)
    lane = iota((1, LANES), 1)
    own = jnp.sum(jnp.where(lane < GENES, summed, 0.0), axis=1, keepdims=True)
    own = jnp.broadcast_to(own, (1, LANES))
    own_ref[...] = own
    copies = []
    for off in range(1, genes):
        copies.append(
            pltpu.make_async_remote_copy(
                src_ref=own_ref,
                dst_ref=gene_buf.at[group],
                send_sem=gene_send.at[off],
                recv_sem=gene_recv.at[off],
                device_id={"gene": lax.rem(group + off, genes)},
            )
        )
    for copy in copies:
        copy.start()
    gene_buf[group] = own
    gene_ref[...] = (summed / counts)[:, 0:GENES]
    for copy in copies:
        copy.wait()
    total = gene_buf[0]
    for at in range(1, genes):
        total = total + gene_buf[at]
    total_ref[...] = total[:, 0:1] * (1.0 / scale)


def over_devices(part, genes, sites, scale):
    vmem = pl.BlockSpec(memory_space=pltpu.VMEM)
    return pl.pallas_call(
        functools.partial(sum_kernel, genes, sites, scale),
        name="over_devices",
        out_shape=(
            jax.ShapeDtypeStruct((1, GENES), F32),
            jax.ShapeDtypeStruct((1, 1), F32),
        ),
        in_specs=[vmem],
        out_specs=(vmem, vmem),
        scratch_shapes=[
            pltpu.VMEM((sites, 1, LANES), F32),
            pltpu.VMEM((genes, 1, LANES), F32),
            pltpu.VMEM((1, LANES), F32),
            pltpu.SemaphoreType.DMA((sites,)),
            pltpu.SemaphoreType.DMA((sites,)),
            pltpu.SemaphoreType.DMA((genes,)),
            pltpu.SemaphoreType.DMA((genes,)),
        ],
        compiler_params=pltpu.CompilerParams(collective_id=0, has_side_effects=True),
    )(part)


def solution(mesh):
    genes, sites = mesh.shape["gene"], mesh.shape["site"]

    def on_device(tips, exchange, freqs, rates, branch, children, slot_gene, site_count):
        values, part = local_part(
            tips, exchange, freqs, rates, branch, children, slot_gene, site_count
        )
        scale = tips.shape[3] * sites
        gene_loglik, total = over_devices(part, genes, sites, scale)
        return values, gene_loglik, total.reshape(())

    pair = P("gene", "site")
    return jax.shard_map(
        on_device,
        mesh=mesh,
        in_specs=(P("gene", None, None, "site"), P(), P(), P(), P(), P(), pair, pair),
        out_specs=(pair, P("gene", None), P()),
        check_vma=False,
    )
```

profile of v0, /device:TPU:1, one launch (start us, length us, event | category | flops | bytes accessed | tf_op | source)
XLA Modules:
  0.0 56.1 jit_solution(16678623292338368588)
XLA Ops:
  0.6 34.9 %local_part.1 = (f32[1,2048]{1,0:T(1,128)}, f32[1,128]{1,0:T(1,128)}) custom-call(s32[2,31]{1,0:T(2,128)} %bitcast.4, s32[1,16]{1,0:T(1,128)} %gene_ref.1, s32[1,16]{1,0:T(1,128)} %count_ref.1, f32[20]{0:T(128)} %freqs_ref.1, f32[4]{0:T(128)} %rates_ref.1, f32[62]{0:T(128)} %branch_ref.1, f32[20,20]{1,0:T(8,128)} %exchange_ref.1, ...), custom_call_target="tpu_custom_call" | custom-call | tf_op jit(solution)/shard_map/local_part/pallas_call | solution.py:265
  35.6 17.7 %over_devices.1 = (f32[1,64]{1,0:T(1,128)}, f32[1,1]{1,0:T(1,128)}) custom-call(f32[1,128]{1,0:T(1,128)} %get-tuple-element.8.part_ref), custom_call_target="tpu_custom_call" | custom-call | tf_op jit(solution)/shard_map/over_devices/pallas_call | solution.py:348
  53.2 1.1 %copy.13 = f32[1,64]{1,0:T(1,128)} copy(f32[1,64]{1,0:T(1,128)} %get-tuple-element.15) | data formatting | bytes 512
where the time goes:
time: 56.3 us; the launch traced here: 56.1 us
  Pallas kernels  52.6 us (93%)
  between operations  2.41 us (4%)
  local copies, waits for them, and re-layouts  1.14 us (2%)
    pallas_call x1, Pallas kernels, local_part(): pl.pallas_call(local_kernel, name='local_part', out_shape=(jax.ShapeDtype...  34.9 us
    pallas_call x1, Pallas kernels, over_devices(): pl.pallas_call(functools.partial(sum_kernel, genes, sites, scale), name='...  17.7 us
    unnamed x1, local copies, waits for them, and re-layouts  1.14 us

commit v1 on v0

v1 whole, which is shorter than its diff:
```python
import functools

import jax
import jax.numpy as jnp
from jax import lax
from jax.experimental import pallas as pl
from jax.experimental.pallas import tpu as pltpu
from jax.sharding import PartitionSpec as P

STATES = 20
RATES = 4
ROWS = STATES * RATES
LEAVES = 32
INNER = 30
NODES = 62
GENES = 64
PAD = 24
LANES = 128
SPLIT = 32
BLOCK = 512
SPREAD = ROWS + 1
FLAT = PAD + 1
F32 = jnp.float32
BF16 = jnp.bfloat16


def iota(shape, axis):
    return lax.broadcasted_iota(jnp.int32, shape, axis)


def rate_powers(exchange_ref, freqs_ref, pad_ref):
    pad_ref[...] = jnp.zeros((LANES, LANES), F32)
    pad_ref[0:STATES, 0:STATES] = exchange_ref[...]
    full = pad_ref[...]
    both = (full + full.T)[0:PAD, :]
    shape = (PAD, LANES)
    sub, lane = iota(shape, 0), iota(shape, 1)
    pi_sub = jnp.zeros(shape, F32)
    pi_lane = jnp.zeros(shape, F32)
    for state in range(STATES):
        value = freqs_ref[state]
        pi_sub = jnp.where(sub == state, value, pi_sub)
        pi_lane = jnp.where(lane == state, value, pi_lane)
    total = jnp.sum(pi_sub, axis=0, keepdims=True)
    pi_sub = pi_sub / total
    pi_lane = pi_lane / total
    off = jnp.where(sub == lane, 0.0, both * 0.5 * pi_sub)
    out_rate = jnp.sum(off, axis=0, keepdims=True)
    mean_rate = jnp.sum(out_rate * pi_lane[0:1], axis=1, keepdims=True)
    gen = (off - jnp.where(sub == lane, out_rate, 0.0)) / mean_rate

    def times(left, right):
        acc = left[:, 0:1] * right[0:1, :]
        for mid in range(1, STATES):
            acc = acc + left[:, mid : mid + 1] * right[mid : mid + 1, :]
        return acc

    second = times(gen, gen) * 0.5
    third = times(second, gen) * (1.0 / 3.0)
    fourth = times(second, second) * (4.0 / 24.0)
    powers = [gen, second, third, fourth]
    for order, part in ((5, gen), (6, second), (7, third), (8, fourth)):
        ratio = {5: 24.0 / 120.0, 6: 48.0 / 720.0, 7: 144.0 / 5040.0, 8: 576.0 / 40320.0}[order]
        powers.append(times(fourth, part) * ratio)
    return powers, pi_sub


def transitions(powers, rates_ref, branch_ref, mat_ref):
    shape = (1, LANES)
    lane = iota(shape, 1)
    category = lane // SPLIT
    rate = jnp.zeros(shape, F32)
    mean = jnp.zeros(shape, F32)
    for k in range(RATES):
        rate = jnp.where(category == k, rates_ref[k], rate)
        mean = mean + rates_ref[k]
    rate = rate / (mean / RATES)
    taus = []
    for half in range(2):
        length = jnp.zeros(shape, F32)
        for at in range(min(SPLIT, NODES - half * SPLIT)):
            length = jnp.where(lane % SPLIT == at, branch_ref[half * SPLIT + at], length)
        taus.append(length * rate / 256.0)
    sub = iota((PAD, LANES), 0)
    for i in range(STATES):
        columns = [jnp.broadcast_to(p[:, i : i + 1], (PAD, LANES)) for p in powers]
        eye = jnp.where(sub == i, 1.0, 0.0)
        for half in range(2):
            acc = columns[7]
            for order in range(6, -1, -1):
                acc = columns[order] + acc * taus[half]
            mat_ref[0, half, i * PAD : (i + 1) * PAD, :] = eye + acc * taus[half]

    def square(step, carry):
        src = lax.rem(step, 2)
        dst = 1 - src
        for half in range(2):
            for first in range(0, STATES, 4):
                accs = [None] * 4
                for mid in range(STATES):
                    row = mat_ref[src, half, mid * PAD : (mid + 1) * PAD, :]
                    for at in range(4):
                        where = (first + at) * PAD + mid
                        factor = mat_ref[src, half, where : where + 1, :]
                        term = factor * row
                        accs[at] = term if accs[at] is None else accs[at] + term
                for at in range(4):
                    start = (first + at) * PAD
                    mat_ref[dst, half, start : start + PAD, :] = accs[at]
        return carry

    lax.fori_loop(0, 8, square, 0)


def operands(children_ref, mat_ref, spread_ref, leaf_ref, inner_ref):
    for half in range(2):
        for group in range(4):
            block = mat_ref[0, half, group * 120 : group * 120 + LANES, :].T
            for at in range(5):
                i = group * 5 + at
                moved = block if at == 0 else pltpu.roll(block, LANES - PAD * at, 1)
                for k in range(RATES):
                    rows = pl.ds(i * RATES + k, SPLIT, stride=SPREAD)
                    spread_ref[half, rows, :] = moved[k * SPLIT : (k + 1) * SPLIT]

    lane = iota((ROWS, LANES), 1)

    def parts(half, at):
        value = spread_ref[half, pl.ds(at * SPREAD, ROWS), :]
        value = jnp.where(lane < STATES, value, 0.0)
        high = value.astype(BF16).astype(F32)
        return high, value - high

    for node in range(LEAVES // 2):
        high, low = parts(0, children_ref[0, node])
        leaf_ref[node, 0:ROWS, :] = (high + pltpu.roll(low, 32, 1)).astype(BF16)
        high, low = parts(0, children_ref[1, node])
        leaf_ref[node, ROWS : 2 * ROWS, :] = (
            pltpu.roll(high, 64, 1) + pltpu.roll(low, 96, 1)
        ).astype(BF16)

    row, col = iota((LANES, 256), 0), iota((LANES, 256), 1)
    state = lax.rem(col, ROWS) // RATES
    low_part = (col >= 2 * ROWS).astype(jnp.int32) * 32
    place = jnp.where((row == state + low_part) & (col < 3 * ROWS), 1.0, 0.0).astype(BF16)
    row, col = iota((ROWS, 256), 0), iota((ROWS, 256), 1)
    same = lax.rem(row, RATES) == lax.rem(col, RATES)
    for at in range(INNER):
        node = LEAVES // 2 + at // 2
        child = jnp.clip(children_ref[at % 2, node] - LEAVES, 0, INNER - 1)
        high, low = parts(1, child)
        both = (high + pltpu.roll(low, 32, 1)).astype(BF16)
        wide = jnp.dot(both, place, preferred_element_type=F32)
        inner_ref[at] = jnp.where(same, wide, 0.0).astype(BF16)


def prune_block(start, tips_ref, children_ref, leaf_ref, inner_ref, flat_ref, level_refs, weight):
    tiles = BLOCK // LANES
    for tile in range(tiles):
        lanes = pl.ds(start + tile * LANES, LANES)
        for state in range(STATES):
            rows = pl.ds(state, LEAVES, stride=FLAT)
            flat_ref[tile, rows, :] = tips_ref[state, :, lanes].astype(F32)

    def keep(ref, at, value):
        high = value.astype(BF16)
        ref[at, 0:ROWS, :] = high
        ref[at, ROWS : 2 * ROWS, :] = (value - high.astype(F32)).astype(BF16)

    filler = jnp.zeros((SPLIT - PAD, BLOCK), F32)

    def leaf(at):
        rows = pl.ds(at * FLAT, PAD)
        value = jnp.concatenate([flat_ref[tile, rows, :] for tile in range(tiles)], axis=1)
        return jnp.concatenate([value, filler], axis=0).astype(BF16)

    for node in range(LEAVES // 2):
        left = leaf(children_ref[0, node])
        right = leaf(children_ref[1, node])
        stacked = jnp.concatenate([left, left, right, right], axis=0)
        both = jnp.dot(leaf_ref[node], stacked, preferred_element_type=F32)
        keep(level_refs[0], node, both[0:ROWS] * both[ROWS:])

    def moved(at, ref, child):
        high = ref[child, 0:ROWS, :]
        low = ref[child, ROWS : 2 * ROWS, :]
        stacked = jnp.concatenate([high, low, high, high[0:16]], axis=0)
        return jnp.dot(inner_ref[at], stacked, preferred_element_type=F32)

    scale = jnp.zeros((1, BLOCK), F32)
    node = LEAVES // 2
    begin = LEAVES
    for level, count in enumerate((8, 4, 2, 1)):
        ref = level_refs[level]
        for place in range(count):
            left = jnp.clip(children_ref[0, node] - begin, 0, 2 * count - 1)
            right = jnp.clip(children_ref[1, node] - begin, 0, 2 * count - 1)
            at = 2 * node - LEAVES
            value = moved(at, ref, left) * moved(at + 1, ref, right)
            if count == 4:
                top = jnp.max(value, axis=0, keepdims=True)
                value = value * (1.0 / top)
                scale = scale + jnp.log(top)
            if count > 1:
                keep(level_refs[level + 1], place, value)
            node = node + 1
        begin = begin + 2 * count
    lik = jnp.sum(value * weight, axis=0, keepdims=True)
    return jnp.log(lik) + scale


def exchange(axis, size, own_ref, buf, send, recv):
    me = lax.axis_index(axis)
    copies = []
    for off in range(1, size):
        copies.append(
            pltpu.make_async_remote_copy(
                src_ref=own_ref,
                dst_ref=buf.at[me],
                send_sem=send.at[off],
                recv_sem=recv.at[off],
                device_id={axis: lax.rem(me + off, size)},
            )
        )
    for copy in copies:
        copy.start()
    buf[me] = own_ref[...]
    return copies


def total_of(copies, buf, size):
    for copy in copies:
        copy.wait()
    summed = buf[0]
    for at in range(1, size):
        summed = summed + buf[at]
    return summed


def kernel(
    mesh_shape,
    scale,
    children_ref,
    gene_ref,
    count_ref,
    freqs_ref,
    rates_ref,
    branch_ref,
    exchange_ref,
    tips_hbm,
    site_ref,
    mean_ref,
    total_ref,
    tips_ref,
    pad_ref,
    mat_ref,
    spread_ref,
    leaf_ref,
    inner_ref,
    flat_ref,
    level_refs,
    weight_ref,
    part_ref,
    own_ref,
    site_buf,
    gene_buf,
    fetch_sem,
    site_sems,
    gene_sems,
):
    genes, sites = mesh_shape
    barrier = pltpu.get_barrier_semaphore()
    for axis, size in (("site", sites), ("gene", genes)):
        for off in range(1, size):
            peer = lax.rem(lax.axis_index(axis) + off, size)
            pl.semaphore_signal(barrier, inc=1, device_id={axis: peer})
    fetch = pltpu.make_async_copy(tips_hbm.at[0], tips_ref, fetch_sem)
    fetch.start()
    powers, pi_sub = rate_powers(exchange_ref, freqs_ref, pad_ref)
    for i in range(STATES):
        row = jnp.broadcast_to(pi_sub[i : i + 1, 0:1] / RATES, (RATES, LANES))
        weight_ref[i * RATES : (i + 1) * RATES, :] = row
    transitions(powers, rates_ref, branch_ref, mat_ref)
    operands(children_ref, mat_ref, spread_ref, leaf_ref, inner_ref)
    part_ref[...] = jnp.zeros((1, LANES), F32)
    for tile in range(BLOCK // LANES):
        flat_ref[tile] = jnp.zeros((LEAVES * FLAT, LANES), F32)
    fetch.wait()
    lane = iota((1, LANES), 1)

    def step(number, carry):
        start = pl.multiple_of(number * BLOCK, BLOCK)
        weight = weight_ref[:, 0:1]
        values = prune_block(
            start, tips_ref, children_ref, leaf_ref, inner_ref, flat_ref, level_refs, weight
        )
        for at in range(BLOCK // LANES):
            slot = number * (BLOCK // LANES) + at
            live = count_ref[0, slot]
            gene = gene_ref[0, slot]
            part = values[:, at * LANES : (at + 1) * LANES]
            part = jnp.where(lane < live, part, 0.0)
            site_ref[:, pl.ds(start + at * LANES, LANES)] = part
            summed = jnp.sum(part, axis=1, keepdims=True)
            add = jnp.where(lane == gene, summed, 0.0)
            add = add + jnp.where(lane == gene + GENES, live.astype(F32), 0.0)
            part_ref[...] = part_ref[...] + add
        return carry

    lax.fori_loop(0, site_ref.shape[1] // BLOCK, step, 0)
    pl.semaphore_wait(barrier, sites + genes - 2)
    copies = exchange("site", sites, part_ref, site_buf, site_sems.at[0], site_sems.at[1])
    summed = total_of(copies, site_buf, sites)
    own = jnp.sum(jnp.where(lane < GENES, summed, 0.0), axis=1, keepdims=True)
    own_ref[...] = jnp.broadcast_to(own, (1, LANES))
    copies = exchange("gene", genes, own_ref, gene_buf, gene_sems.at[0], gene_sems.at[1])
    mean_ref[...] = (summed / pltpu.roll(summed, GENES, 1))[:, 0:GENES]
    total_ref[...] = total_of(copies, gene_buf, genes)[:, 0:1] * (1.0 / scale)


def likelihoods(genes, width, tips, exchange_, freqs, rates, branch, children, slot_gene, site_count):
    sites = tips.shape[3]
    smem = pl.BlockSpec(memory_space=pltpu.SMEM)
    vmem = pl.BlockSpec(memory_space=pltpu.VMEM)
    return pl.pallas_call(
        functools.partial(kernel, (genes, width), sites * width),
        name="likelihoods",
        out_shape=(
            jax.ShapeDtypeStruct((1, sites), F32),
            jax.ShapeDtypeStruct((1, GENES), F32),
            jax.ShapeDtypeStruct((1, 1), F32),
        ),
        in_specs=[smem] * 6 + [vmem, pl.BlockSpec(memory_space=pl.ANY)],
        out_specs=(vmem, vmem, vmem),
        scratch_shapes=[
            pltpu.VMEM((STATES, LEAVES, sites), BF16),
            pltpu.VMEM((LANES, LANES), F32),
            pltpu.VMEM((2, 2, 512, LANES), F32),
            pltpu.VMEM((2, SPLIT * SPREAD, LANES), F32),
            pltpu.VMEM((LEAVES // 2, 2 * ROWS, LANES), BF16),
            pltpu.VMEM((INNER, ROWS, 256), BF16),
            pltpu.VMEM((BLOCK // LANES, FLAT * LEAVES, LANES), F32),
            [pltpu.VMEM((count, 2 * ROWS, BLOCK), BF16) for count in (16, 8, 4, 2)],
            pltpu.VMEM((ROWS, LANES), F32),
            pltpu.VMEM((1, LANES), F32),
            pltpu.VMEM((1, LANES), F32),
            pltpu.VMEM((width, 1, LANES), F32),
            pltpu.VMEM((genes, 1, LANES), F32),
            pltpu.SemaphoreType.DMA,
            pltpu.SemaphoreType.DMA((2, width)),
            pltpu.SemaphoreType.DMA((2, genes)),
        ],
        compiler_params=pltpu.CompilerParams(
            vmem_limit_bytes=60 * 1024 * 1024, collective_id=0, has_side_effects=True
        ),
    )(
        children.T,
        slot_gene,
        site_count,
        freqs,
        rates,
        branch,
        exchange_,
        tips.transpose(0, 2, 1, 3),
    )


def solution(mesh):
    genes, sites = mesh.shape["gene"], mesh.shape["site"]

    def on_device(*args):
        values, gene_loglik, total = likelihoods(genes, sites, *args)
        return values, gene_loglik, total.reshape(())

    pair = P("gene", "site")
    return jax.shard_map(
        on_device,
        mesh=mesh,
        in_specs=(P("gene", None, None, "site"), P(), P(), P(), P(), P(), pair, pair),
        out_specs=(pair, P("gene", None), P()),
        check_vma=False,
    )
```

time: 56.3 us -> 41.6 us (0.74)
  Pallas kernels: 52.6 us -> 36.5 us
  local copies, waits for them, and re-layouts: 1.14 us -> 2.43 us
    pallas_call x2 -> x1, Pallas kernels: 52.6 us -> 36.5 us  [likelihoods(): pl.pallas_call(functools.partial(kernel, (genes, width), sites * width),...]
    unnamed x1 -> x2, local copies, waits for them, and re-layouts: 1.14 us -> 2.43 us
where the time goes in v1:
time: 41.6 us; the launch traced here: 41.3 us
  Pallas kernels  36.5 us (88%)
  local copies, waits for them, and re-layouts  2.43 us (6%)
  between operations  2.4 us (6%)
    pallas_call x1, Pallas kernels, likelihoods(): pl.pallas_call(functools.partial(kernel, (genes, width), sites * width),...  36.5 us
    unnamed x2, local copies, waits for them, and re-layouts  2.43 us

profile of v1, /device:TPU:1, one launch (start us, length us, event | category | flops | bytes accessed | tf_op | source)
XLA Modules:
  0.0 41.3 jit_solution(13028135041541573485)
XLA Ops:
  0.6 36.5 %likelihoods.1 = (f32[1,2048]{1,0:T(1,128)}, f32[1,64]{1,0:T(1,128)}, f32[1,1]{1,0:T(1,128)}) custom-call(s32[2,31]{1,0:T(2,128)} %bitcast.4, s32[1,16]{1,0:T(1,128)} %gene_ref.1, s32[1,16]{1,0:T(1,128)} %count_ref.1, f32[20]{0:T(128)} %freqs_ref.1, f32[4]{0:T(128)} %rates_ref.1, f32[62]{0:T(128)} %branch_ref.1, f32[20,20]{1,0:T(8,128)} %exchange_ref.1, ...), custom_call_target="tpu_custom_call" | custom-call | tf_op jit(solution)/shard_map/likelihoods/pallas_call | solution.py:325
  37.1 1.3 %copy.14 = f32[1,2048]{1,0:T(1,128)} copy(f32[1,2048]{1,0:T(1,128)} %get-tuple-element.12) | data formatting | bytes 16384
  38.4 1.1 %copy.15 = f32[1,64]{1,0:T(1,128)} copy(f32[1,64]{1,0:T(1,128)} %get-tuple-element.13) | data formatting | bytes 512

commit v2 on v1

v2 whole, which is shorter than its diff:
```python
import functools

import jax
import jax.numpy as jnp
from jax import lax
from jax.experimental import pallas as pl
from jax.experimental.pallas import tpu as pltpu
from jax.sharding import PartitionSpec as P

STATES = 20
RATES = 4
ROWS = STATES * RATES
LEAVES = 32
INNER = 30
NODES = 62
GENES = 64
PAD = 24
LANES = 128
SPLIT = 32
CHUNK = 256
LEVEL_NODES = (16, 8, 4, 2)
SQUARINGS = 8
SPREAD = ROWS + 1
FLAT = PAD + 1
F32 = jnp.float32
BF16 = jnp.bfloat16


def iota(shape, axis):
    return lax.broadcasted_iota(jnp.int32, shape, axis)


def rate_powers(exchange_ref, freqs_ref, pad_ref):
    pad_ref[...] = jnp.zeros((LANES, LANES), F32)
    pad_ref[0:STATES, 0:STATES] = exchange_ref[...]
    full = pad_ref[...]
    both = (full + full.T)[0:PAD, :]
    shape = (PAD, LANES)
    sub, lane = iota(shape, 0), iota(shape, 1)
    pi_sub = jnp.zeros(shape, F32)
    pi_lane = jnp.zeros(shape, F32)
    for state in range(STATES):
        value = freqs_ref[state]
        pi_sub = jnp.where(sub == state, value, pi_sub)
        pi_lane = jnp.where(lane == state, value, pi_lane)
    total = jnp.sum(pi_sub, axis=0, keepdims=True)
    pi_sub = pi_sub / total
    pi_lane = pi_lane / total
    off = jnp.where(sub == lane, 0.0, both * 0.5 * pi_sub)
    out_rate = jnp.sum(off, axis=0, keepdims=True)
    mean_rate = jnp.sum(out_rate * pi_lane[0:1], axis=1, keepdims=True)
    gen = (off - jnp.where(sub == lane, out_rate, 0.0)) / mean_rate

    def times(left, right):
        acc = left[:, 0:1] * right[0:1, :]
        for mid in range(1, STATES):
            acc = acc + left[:, mid : mid + 1] * right[mid : mid + 1, :]
        return acc

    second = times(gen, gen) * 0.5
    third = times(second, gen) * (1.0 / 3.0)
    fourth = times(second, second) * (4.0 / 24.0)
    powers = [gen, second, third, fourth]
    for order, part in ((5, gen), (6, second), (7, third), (8, fourth)):
        ratio = {5: 24.0 / 120.0, 6: 48.0 / 720.0, 7: 144.0 / 5040.0, 8: 576.0 / 40320.0}[order]
        powers.append(times(fourth, part) * ratio)
    return powers, pi_sub


def taylor(powers, rates_ref, branch_ref, mat_ref):
    shape = (1, LANES)
    lane = iota(shape, 1)
    category = lane // SPLIT
    rate = jnp.zeros(shape, F32)
    mean = jnp.zeros(shape, F32)
    for k in range(RATES):
        rate = jnp.where(category == k, rates_ref[k], rate)
        mean = mean + rates_ref[k]
    rate = rate / (mean / RATES)
    taus = []
    for half in range(2):
        length = jnp.zeros(shape, F32)
        for at in range(min(SPLIT, NODES - half * SPLIT)):
            length = jnp.where(lane % SPLIT == at, branch_ref[half * SPLIT + at], length)
        taus.append(length * rate / 256.0)
    sub = iota((PAD, LANES), 0)
    for i in range(STATES):
        columns = [jnp.broadcast_to(p[:, i : i + 1], (PAD, LANES)) for p in powers]
        eye = jnp.where(sub == i, 1.0, 0.0)
        for half in range(2):
            acc = columns[7]
            for order in range(6, -1, -1):
                acc = columns[order] + acc * taus[half]
            mat_ref[0, half, i * PAD : (i + 1) * PAD, :] = eye + acc * taus[half]


def square(step, half, mat_ref, beside=None):
    src = lax.rem(step, 2)
    dst = 1 - src
    for first in range(0, STATES, 4):
        if beside is not None:
            beside(first // 4)
        accs = [None] * 4
        for mid in range(STATES):
            row = mat_ref[src, half, mid * PAD : (mid + 1) * PAD, :]
            for at in range(4):
                where = (first + at) * PAD + mid
                factor = mat_ref[src, half, where : where + 1, :]
                term = factor * row
                accs[at] = term if accs[at] is None else accs[at] + term
        for at in range(4):
            start = (first + at) * PAD
            mat_ref[dst, half, start : start + PAD, :] = accs[at]


def tree_order(children_ref, order_ref):
    place = NODES
    parents = [NODES]
    for count in (2, 4, 8, 16, 32):
        place = place - count
        ids = []
        for at, parent in enumerate(parents):
            row = jnp.clip(parent - LEAVES, 0, NODES - LEAVES)
            for side in range(2):
                child = children_ref[side, row]
                order_ref[place + 2 * at + side] = child
                ids.append(child)
        parents = ids


def spread(half, mat_ref, spread_ref):
    for group in range(4):
        block = mat_ref[0, half, group * 120 : group * 120 + LANES, :].T
        for at in range(5):
            i = group * 5 + at
            moved = block if at == 0 else pltpu.roll(block, LANES - PAD * at, 1)
            for k in range(RATES):
                rows = pl.ds(i * RATES + k, SPLIT, stride=SPREAD)
                spread_ref[half, rows, :] = moved[k * SPLIT : (k + 1) * SPLIT]


def parts(half, at, spread_ref):
    value = spread_ref[half, pl.ds(at * SPREAD, ROWS), :]
    value = jnp.where(iota((ROWS, LANES), 1) < STATES, value, 0.0)
    high = value.astype(BF16).astype(F32)
    return high, value - high


def leaf_operands(order_ref, spread_ref, leaf_ref):
    for node in range(LEAVES // 2):
        high, low = parts(0, jnp.clip(order_ref[2 * node], 0, LEAVES - 1), spread_ref)
        leaf_ref[node, 0:ROWS, :] = (high + pltpu.roll(low, 32, 1)).astype(BF16)
        high, low = parts(0, jnp.clip(order_ref[2 * node + 1], 0, LEAVES - 1), spread_ref)
        leaf_ref[node, ROWS : 2 * ROWS, :] = (
            pltpu.roll(high, 64, 1) + pltpu.roll(low, 96, 1)
        ).astype(BF16)


def inner_operands(order_ref, spread_ref, inner_ref):
    row, col = iota((LANES, 256), 0), iota((LANES, 256), 1)
    state = lax.rem(col, ROWS) // RATES
    low_part = (col >= 2 * ROWS).astype(jnp.int32) * 32
    place = jnp.where((row == state + low_part) & (col < 3 * ROWS), 1.0, 0.0).astype(BF16)
    row, col = iota((ROWS, 256), 0), iota((ROWS, 256), 1)
    same = lax.rem(row, RATES) == lax.rem(col, RATES)
    for at in range(INNER):
        child = jnp.clip(order_ref[LEAVES + at] - LEAVES, 0, INNER - 1)
        high, low = parts(1, child, spread_ref)
        both = (high + pltpu.roll(low, 32, 1)).astype(BF16)
        wide = jnp.dot(both, place, preferred_element_type=F32)
        inner_ref[at] = jnp.where(same, wide, 0.0).astype(BF16)


def gather_leaves(chunk, tips_ref, order_ref, flat_ref, leaves_ref):
    tiles = CHUNK // LANES
    for tile in range(tiles):
        lanes = pl.ds(pl.multiple_of(chunk * CHUNK, CHUNK) + tile * LANES, LANES)
        for state in range(STATES):
            rows = pl.ds(state, LEAVES, stride=FLAT)
            flat_ref[tile, rows, :] = tips_ref[state, :, lanes].astype(F32)
    filler = jnp.zeros((SPLIT - PAD, CHUNK), F32)
    for at in range(LEAVES):
        rows = pl.ds(jnp.clip(order_ref[at], 0, LEAVES - 1) * FLAT, PAD)
        value = jnp.concatenate([flat_ref[tile, rows, :] for tile in range(tiles)], axis=1)
        value = jnp.concatenate([value, filler], axis=0).astype(BF16)
        leaves_ref[chunk, at * SPLIT : (at + 1) * SPLIT, :] = value


def keep(ref, chunk, at, value):
    high = value.astype(BF16)
    ref[chunk, at, 0:ROWS, :] = high
    ref[chunk, at, ROWS : 2 * ROWS, :] = (value - high.astype(F32)).astype(BF16)


def prune_leaves(nodes, chunk, leaves_ref, leaf_ref, level_ref):
    for node in nodes:
        left = leaves_ref[chunk, 2 * node * SPLIT : (2 * node + 1) * SPLIT, :]
        right = leaves_ref[chunk, (2 * node + 1) * SPLIT : (2 * node + 2) * SPLIT, :]
        stacked = jnp.concatenate([left, left, right, right], axis=0)
        both = jnp.dot(leaf_ref[node], stacked, preferred_element_type=F32)
        keep(level_ref, chunk, node, both[0:ROWS] * both[ROWS:])


def prune_inner(chunks, inner_ref, level_refs, weight):
    def moved(at, ref, chunk, child):
        high = ref[chunk, child, 0:ROWS, :]
        low = ref[chunk, child, ROWS : 2 * ROWS, :]
        stacked = jnp.concatenate([high, low, high], axis=0)
        return jnp.dot(inner_ref[at, :, 0 : 3 * ROWS], stacked, preferred_element_type=F32)

    scales = [jnp.zeros((1, CHUNK), F32) for _ in range(chunks)]
    results = []
    base = 0
    for level, count in enumerate(LEVEL_NODES):
        ref = level_refs[level]
        parents = count // 2
        for chunk in range(chunks):
            for place in range(parents):
                at = base + 2 * place
                value = moved(at, ref, chunk, 2 * place) * moved(at + 1, ref, chunk, 2 * place + 1)
                if parents == 4:
                    top = jnp.max(value, axis=0, keepdims=True)
                    value = value * (1.0 / top)
                    scales[chunk] = scales[chunk] + jnp.log(top)
                if parents > 1:
                    keep(level_refs[level + 1], chunk, place, value)
                else:
                    lik = jnp.sum(value * weight, axis=0, keepdims=True)
                    results.append(jnp.log(lik) + scales[chunk])
        base = base + count
    return results


def exchange(axis, size, own_ref, buf, send, recv):
    me = lax.axis_index(axis)
    copies = []
    for off in range(1, size):
        copies.append(
            pltpu.make_async_remote_copy(
                src_ref=own_ref,
                dst_ref=buf.at[me],
                send_sem=send.at[off],
                recv_sem=recv.at[off],
                device_id={axis: lax.rem(me + off, size)},
            )
        )
    for copy in copies:
        copy.start()
    buf[me] = own_ref[...]
    return copies


def total_of(copies, buf, size):
    for copy in copies:
        copy.wait()
    summed = buf[0]
    for at in range(1, size):
        summed = summed + buf[at]
    return summed


def kernel(
    mesh_shape,
    scale,
    children_ref,
    gene_ref,
    count_ref,
    freqs_ref,
    rates_ref,
    branch_ref,
    exchange_ref,
    tips_hbm,
    site_ref,
    mean_ref,
    total_ref,
    tips_ref,
    order_ref,
    leaves_ref,
    pad_ref,
    mat_ref,
    spread_ref,
    leaf_ref,
    inner_ref,
    flat_ref,
    level_refs,
    weight_ref,
    part_ref,
    own_ref,
    site_buf,
    gene_buf,
    fetch_sems,
    site_sems,
    gene_sems,
):
    genes, sites = mesh_shape
    barrier = pltpu.get_barrier_semaphore()
    for axis, size in (("site", sites), ("gene", genes)):
        for off in range(1, size):
            peer = lax.rem(lax.axis_index(axis) + off, size)
            pl.semaphore_signal(barrier, inc=1, device_id={axis: peer})
    chunks = site_ref.shape[1] // CHUNK

    def fetch(chunk):
        lanes = pl.ds(pl.multiple_of(chunk * CHUNK, CHUNK), CHUNK)
        return pltpu.make_async_copy(
            tips_hbm.at[0, :, :, lanes], tips_ref.at[:, :, lanes], fetch_sems.at[chunk]
        )

    for chunk in range(chunks):
        fetch(chunk).start()
    tree_order(children_ref, order_ref)
    for tile in range(CHUNK // LANES):
        flat_ref[tile] = jnp.zeros((LEAVES * FLAT, LANES), F32)
    powers, pi_sub = rate_powers(exchange_ref, freqs_ref, pad_ref)
    for i in range(STATES):
        row = jnp.broadcast_to(pi_sub[i : i + 1, 0:1] / RATES, (RATES, LANES))
        weight_ref[i * RATES : (i + 1) * RATES, :] = row

    taylor(powers, rates_ref, branch_ref, mat_ref)
    per_step = chunks // SQUARINGS

    def leaf_branches(step, carry):
        for at in range(per_step):
            chunk = step * per_step + at
            fetch(chunk).wait()
            gather_leaves(chunk, tips_ref, order_ref, flat_ref, leaves_ref)
        square(step, 0, mat_ref)
        return carry

    lax.fori_loop(0, SQUARINGS, leaf_branches, 0)
    spread(0, mat_ref, spread_ref)
    leaf_operands(order_ref, spread_ref, leaf_ref)

    def inner_branches(step, carry):
        def beside(number):
            for at in range(per_step):
                nodes = range(LEAVES // 2 * number // 5, LEAVES // 2 * (number + 1) // 5)
                prune_leaves(nodes, step * per_step + at, leaves_ref, leaf_ref, level_refs[0])

        square(step, 1, mat_ref, beside)
        return carry

    lax.fori_loop(0, SQUARINGS, inner_branches, 0)
    spread(1, mat_ref, spread_ref)
    inner_operands(order_ref, spread_ref, inner_ref)
    results = prune_inner(chunks, inner_ref, level_refs, weight_ref[:, 0:1])
    lane = iota((1, LANES), 1)
    gathered = jnp.zeros((1, LANES), F32)
    for slot in range(chunks * CHUNK // LANES):
        live = count_ref[0, slot]
        gene = gene_ref[0, slot]
        at = slot * LANES % CHUNK
        part = results[slot * LANES // CHUNK][:, at : at + LANES]
        part = jnp.where(lane < live, part, 0.0)
        site_ref[:, slot * LANES : (slot + 1) * LANES] = part
        summed = jnp.sum(part, axis=1, keepdims=True)
        gathered = gathered + jnp.where(lane == gene, summed, 0.0)
        gathered = gathered + jnp.where(lane == gene + GENES, live.astype(F32), 0.0)
    part_ref[...] = gathered
    pl.semaphore_wait(barrier, sites + genes - 2)
    copies = exchange("site", sites, part_ref, site_buf, site_sems.at[0], site_sems.at[1])
    summed = total_of(copies, site_buf, sites)
    own = jnp.sum(jnp.where(lane < GENES, summed, 0.0), axis=1, keepdims=True)
    own_ref[...] = jnp.broadcast_to(own, (1, LANES))
    copies = exchange("gene", genes, own_ref, gene_buf, gene_sems.at[0], gene_sems.at[1])
    mean_ref[...] = (summed / pltpu.roll(summed, GENES, 1))[:, 0:GENES]
    total_ref[...] = total_of(copies, gene_buf, genes)[:, 0:1] * (1.0 / scale)


def likelihoods(genes, width, tips, exchange_, freqs, rates, branch, children, slot_gene, site_count):
    sites = tips.shape[3]
    chunks = sites // CHUNK
    smem = pl.BlockSpec(memory_space=pltpu.SMEM)
    vmem = pl.BlockSpec(memory_space=pltpu.VMEM)
    return pl.pallas_call(
        functools.partial(kernel, (genes, width), sites * width),
        name="likelihoods",
        out_shape=(
            jax.ShapeDtypeStruct((1, sites), F32),
            jax.ShapeDtypeStruct((1, GENES), F32),
            jax.ShapeDtypeStruct((1, 1), F32),
        ),
        in_specs=[smem] * 6 + [vmem, pl.BlockSpec(memory_space=pl.ANY)],
        out_specs=(vmem, vmem, vmem),
        scratch_shapes=[
            pltpu.VMEM((STATES, LEAVES, sites), BF16),
            pltpu.SMEM((NODES,), jnp.int32),
            pltpu.VMEM((chunks, LEAVES * SPLIT, CHUNK), BF16),
            pltpu.VMEM((LANES, LANES), F32),
            pltpu.VMEM((2, 2, 512, LANES), F32),
            pltpu.VMEM((2, SPLIT * SPREAD, LANES), F32),
            pltpu.VMEM((LEAVES // 2, 2 * ROWS, LANES), BF16),
            pltpu.VMEM((INNER, ROWS, 256), BF16),
            pltpu.VMEM((CHUNK // LANES, FLAT * LEAVES, LANES), F32),
            [pltpu.VMEM((chunks, count, 2 * ROWS, CHUNK), BF16) for count in LEVEL_NODES],
            pltpu.VMEM((ROWS, LANES), F32),
            pltpu.VMEM((1, LANES), F32),
            pltpu.VMEM((1, LANES), F32),
            pltpu.VMEM((width, 1, LANES), F32),
            pltpu.VMEM((genes, 1, LANES), F32),
            pltpu.SemaphoreType.DMA((chunks,)),
            pltpu.SemaphoreType.DMA((2, width)),
            pltpu.SemaphoreType.DMA((2, genes)),
        ],
        compiler_params=pltpu.CompilerParams(
            vmem_limit_bytes=60 * 1024 * 1024, collective_id=0, has_side_effects=True
        ),
    )(
        children.T,
        slot_gene,
        site_count,
        freqs,
        rates,
        branch,
        exchange_,
        tips.transpose(0, 2, 1, 3),
    )


def solution(mesh):
    genes, sites = mesh.shape["gene"], mesh.shape["site"]

    def on_device(*args):
        values, gene_loglik, total = likelihoods(genes, sites, *args)
        return values, gene_loglik, total.reshape(())

    pair = P("gene", "site")
    return jax.shard_map(
        on_device,
        mesh=mesh,
        in_specs=(P("gene", None, None, "site"), P(), P(), P(), P(), P(), pair, pair),
        out_specs=(pair, P("gene", None), P()),
        check_vma=False,
    )
```

time: 41.6 us -> 40.3 us (0.969)
  Pallas kernels: 36.5 us -> 35.2 us
    pallas_call x1, Pallas kernels: 36.5 us -> 35.2 us  [likelihoods(): pl.pallas_call(functools.partial(kernel, (genes, width), sites * width),...]
where the time goes in v2:
time: 40.3 us; the launch traced here: 40 us
  Pallas kernels  35.2 us (87%)
  local copies, waits for them, and re-layouts  2.43 us (6%)
  between operations  2.4 us (6%)
    pallas_call x1, Pallas kernels, likelihoods(): pl.pallas_call(functools.partial(kernel, (genes, width), sites * width),...  35.2 us
    unnamed x2, local copies, waits for them, and re-layouts  2.43 us

profile of v2, /device:TPU:1, one launch (start us, length us, event | category | flops | bytes accessed | tf_op | source)
XLA Modules:
  0.0 40.0 jit_solution(1768407306339183943)
XLA Ops:
  0.6 35.2 %likelihoods.1 = (f32[1,2048]{1,0:T(1,128)}, f32[1,64]{1,0:T(1,128)}, f32[1,1]{1,0:T(1,128)}) custom-call(s32[2,31]{1,0:T(2,128)} %bitcast.4, s32[1,16]{1,0:T(1,128)} %gene_ref.1, s32[1,16]{1,0:T(1,128)} %count_ref.1, f32[20]{0:T(128)} %freqs_ref.1, f32[4]{0:T(128)} %rates_ref.1, f32[62]{0:T(128)} %branch_ref.1, f32[20,20]{1,0:T(8,128)} %exchange_ref.1, ...), custom_call_target="tpu_custom_call" | custom-call | tf_op jit(solution)/shard_map/likelihoods/pallas_call | solution.py:375
  35.8 1.3 %copy.14 = f32[1,2048]{1,0:T(1,128)} copy(f32[1,2048]{1,0:T(1,128)} %get-tuple-element.12) | data formatting | bytes 16384
  37.1 1.1 %copy.15 = f32[1,64]{1,0:T(1,128)} copy(f32[1,64]{1,0:T(1,128)} %get-tuple-element.13) | data formatting | bytes 512

commit v3 on v2

--- a/solution.py
+++ b/solution.py
@@ -231,32 +231,8 @@
     return results
 
 
-def exchange(axis, size, own_ref, buf, send, recv):
-    me = lax.axis_index(axis)
-    copies = []
-    for off in range(1, size):
-        copies.append(
-            pltpu.make_async_remote_copy(
-                src_ref=own_ref,
-                dst_ref=buf.at[me],
-                send_sem=send.at[off],
-                recv_sem=recv.at[off],
-                device_id={axis: lax.rem(me + off, size)},
-            )
-        )
-    for copy in copies:
-        copy.start()
-    buf[me] = own_ref[...]
-    return copies
-
-
-def total_of(copies, buf, size):
-    for copy in copies:
-        copy.wait()
-    summed = buf[0]
-    for at in range(1, size):
-        summed = summed + buf[at]
-    return summed
+def peers(genes, sites):
+    return [(g, m) for g in range(genes) for m in range(sites) if g or m]
 
 
 def kernel(
@@ -285,19 +261,19 @@
     level_refs,
     weight_ref,
     part_ref,
-    own_ref,
-    site_buf,
-    gene_buf,
+    rows_ref,
     fetch_sems,
-    site_sems,
-    gene_sems,
+    sems,
 ):
     genes, sites = mesh_shape
     barrier = pltpu.get_barrier_semaphore()
-    for axis, size in (("site", sites), ("gene", genes)):
-        for off in range(1, size):
-            peer = lax.rem(lax.axis_index(axis) + off, size)
-            pl.semaphore_signal(barrier, inc=1, device_id={axis: peer})
+    group, member = lax.axis_index("gene"), lax.axis_index("site")
+
+    def device(gene, site):
+        return (lax.rem(group + gene, genes), lax.rem(member + site, sites))
+
+    for gene, site in peers(genes, sites):
+        pl.semaphore_signal(barrier, inc=1, device_id=device(gene, site))
     chunks = site_ref.shape[1] // CHUNK
 
     def fetch(chunk):
@@ -357,14 +333,34 @@
         gathered = gathered + jnp.where(lane == gene, summed, 0.0)
         gathered = gathered + jnp.where(lane == gene + GENES, live.astype(F32), 0.0)
     part_ref[...] = gathered
-    pl.semaphore_wait(barrier, sites + genes - 2)
-    copies = exchange("site", sites, part_ref, site_buf, site_sems.at[0], site_sems.at[1])
-    summed = total_of(copies, site_buf, sites)
-    own = jnp.sum(jnp.where(lane < GENES, summed, 0.0), axis=1, keepdims=True)
-    own_ref[...] = jnp.broadcast_to(own, (1, LANES))
-    copies = exchange("gene", genes, own_ref, gene_buf, gene_sems.at[0], gene_sems.at[1])
+    pl.semaphore_wait(barrier, genes * sites - 1)
+    copies = []
+    for gene, site in peers(genes, sites):
+        at = gene * sites + site
+        copies.append(
+            pltpu.make_async_remote_copy(
+                src_ref=part_ref,
+                dst_ref=rows_ref.at[group, member],
+                send_sem=sems.at[0, at],
+                recv_sem=sems.at[1, at],
+                device_id=device(gene, site),
+            )
+        )
+    for copy in copies:
+        copy.start()
+    rows_ref[group, member] = gathered
+    for copy in copies:
+        copy.wait()
+    summed = rows_ref[group, 0]
+    for at in range(1, sites):
+        summed = summed + rows_ref[group, at]
     mean_ref[...] = (summed / pltpu.roll(summed, GENES, 1))[:, 0:GENES]
-    total_ref[...] = total_of(copies, gene_buf, genes)[:, 0:1] * (1.0 / scale)
+    total = jnp.zeros((1, LANES), F32)
+    for gene in range(genes):
+        for site in range(sites):
+            total = total + rows_ref[gene, site]
+    total = jnp.sum(jnp.where(lane < GENES, total, 0.0), axis=1, keepdims=True)
+    total_ref[...] = total * (1.0 / scale)
 
 
 def likelihoods(genes, width, tips, exchange_, freqs, rates, branch, children, slot_gene, site_count):
@@ -395,12 +391,9 @@
             [pltpu.VMEM((chunks, count, 2 * ROWS, CHUNK), BF16) for count in LEVEL_NODES],
             pltpu.VMEM((ROWS, LANES), F32),
             pltpu.VMEM((1, LANES), F32),
-            pltpu.VMEM((1, LANES), F32),
-            pltpu.VMEM((width, 1, LANES), F32),
-            pltpu.VMEM((genes, 1, LANES), F32),
+            pltpu.VMEM((genes, width, 1, LANES), F32),
             pltpu.SemaphoreType.DMA((chunks,)),
-            pltpu.SemaphoreType.DMA((2, width)),
-            pltpu.SemaphoreType.DMA((2, genes)),
+            pltpu.SemaphoreType.DMA((2, genes * width)),
         ],
         compiler_params=pltpu.CompilerParams(
             vmem_limit_bytes=60 * 1024 * 1024, collective_id=0, has_side_effects=True

time: 40.3 us -> 41.5 us (1.030)
  Pallas kernels: 35.2 us -> 36.4 us
    pallas_call x1, Pallas kernels: 35.2 us -> 36.4 us  [likelihoods(): pl.pallas_call(functools.partial(kernel, (genes, width), sites * width),...]
where the time goes in v3:
time: 41.5 us; the launch traced here: 41.2 us
  Pallas kernels  36.4 us (88%)
  local copies, waits for them, and re-layouts  2.43 us (6%)
  between operations  2.4 us (6%)
    pallas_call x1, Pallas kernels, likelihoods(): pl.pallas_call(functools.partial(kernel, (genes, width), sites * width),...  36.4 us
    unnamed x2, local copies, waits for them, and re-layouts  2.43 us

profile of v3, /device:TPU:1, one launch (start us, length us, event | category | flops | bytes accessed | tf_op | source)
XLA Modules:
  0.0 41.2 jit_solution(11347290943364554678)
XLA Ops:
  0.6 36.4 %likelihoods.1 = (f32[1,2048]{1,0:T(1,128)}, f32[1,64]{1,0:T(1,128)}, f32[1,1]{1,0:T(1,128)}) custom-call(s32[2,31]{1,0:T(2,128)} %bitcast.4, s32[1,16]{1,0:T(1,128)} %gene_ref.1, s32[1,16]{1,0:T(1,128)} %count_ref.1, f32[20]{0:T(128)} %freqs_ref.1, f32[4]{0:T(128)} %rates_ref.1, f32[62]{0:T(128)} %branch_ref.1, f32[20,20]{1,0:T(8,128)} %exchange_ref.1, ...), custom_call_target="tpu_custom_call" | custom-call | tf_op jit(solution)/shard_map/likelihoods/pallas_call | solution.py:371
  37.0 1.3 %copy.14 = f32[1,2048]{1,0:T(1,128)} copy(f32[1,2048]{1,0:T(1,128)} %get-tuple-element.12) | data formatting | bytes 16384
  38.3 1.1 %copy.15 = f32[1,64]{1,0:T(1,128)} copy(f32[1,64]{1,0:T(1,128)} %get-tuple-element.13) | data formatting | bytes 512

commit v4 on v2

--- a/solution.py
+++ b/solution.py
@@ -261,7 +261,6 @@
 
 def kernel(
     mesh_shape,
-    scale,
     children_ref,
     gene_ref,
     count_ref,
@@ -271,7 +270,7 @@
     exchange_ref,
     tips_hbm,
     site_ref,
-    mean_ref,
+    sums_ref,
     total_ref,
     tips_ref,
     order_ref,
@@ -363,8 +362,8 @@
     own = jnp.sum(jnp.where(lane < GENES, summed, 0.0), axis=1, keepdims=True)
     own_ref[...] = jnp.broadcast_to(own, (1, LANES))
     copies = exchange("gene", genes, own_ref, gene_buf, gene_sems.at[0], gene_sems.at[1])
-    mean_ref[...] = (summed / pltpu.roll(summed, GENES, 1))[:, 0:GENES]
-    total_ref[...] = total_of(copies, gene_buf, genes)[:, 0:1] * (1.0 / scale)
+    sums_ref[...] = summed
+    total_ref[...] = total_of(copies, gene_buf, genes)
 
 
 def likelihoods(genes, width, tips, exchange_, freqs, rates, branch, children, slot_gene, site_count):
@@ -373,12 +372,12 @@
     smem = pl.BlockSpec(memory_space=pltpu.SMEM)
     vmem = pl.BlockSpec(memory_space=pltpu.VMEM)
     return pl.pallas_call(
-        functools.partial(kernel, (genes, width), sites * width),
+        functools.partial(kernel, (genes, width)),
         name="likelihoods",
         out_shape=(
             jax.ShapeDtypeStruct((1, sites), F32),
-            jax.ShapeDtypeStruct((1, GENES), F32),
-            jax.ShapeDtypeStruct((1, 1), F32),
+            jax.ShapeDtypeStruct((1, LANES), F32),
+            jax.ShapeDtypeStruct((1, LANES), F32),
         ),
         in_specs=[smem] * 6 + [vmem, pl.BlockSpec(memory_space=pl.ANY)],
         out_specs=(vmem, vmem, vmem),
@@ -417,11 +416,35 @@
     )
 
 
+def finish_kernel(scale, values_ref, sums_ref, total_ref, site_out, mean_out, total_out):
+    site_out[...] = values_ref[...]
+    sums = sums_ref[...]
+    mean_out[...] = (sums / pltpu.roll(sums, GENES, 1))[:, 0:GENES]
+    total_out[...] = total_ref[:, 0:1] * (1.0 / scale)
+
+
+def finish(values, sums, total, scale):
+    vmem = pl.BlockSpec(memory_space=pltpu.VMEM)
+    return pl.pallas_call(
+        functools.partial(finish_kernel, scale),
+        name="finish",
+        out_shape=(
+            jax.ShapeDtypeStruct(values.shape, F32),
+            jax.ShapeDtypeStruct((1, GENES), F32),
+            jax.ShapeDtypeStruct((1, 1), F32),
+        ),
+        in_specs=[vmem] * 3,
+        out_specs=(vmem, vmem, vmem),
+    )(values, sums, total)
+
+
 def solution(mesh):
     genes, sites = mesh.shape["gene"], mesh.shape["site"]
 
     def on_device(*args):
-        values, gene_loglik, total = likelihoods(genes, sites, *args)
+        values, sums, total = likelihoods(genes, sites, *args)
+        scale = values.shape[1] * sites
+        values, gene_loglik, total = finish(values, sums, total, scale)
         return values, gene_loglik, total.reshape(())
 
     pair = P("gene", "site")

time: 40.3 us -> 37.3 us (0.926)
  local copies, waits for them, and re-layouts: 2.43 us -> 0 us
  between operations: 2.4 us -> 0.64 us
  Pallas kernels: 35.2 us -> 36.5 us
    unnamed x2 -> x0, local copies, waits for them, and re-layouts: 2.43 us -> none
    pallas_call x1 -> x2, Pallas kernels: 35.2 us -> 36.5 us  [the longest x1 35.2 us: likelihoods(): pl.pallas_call(functools.partial(kernel, (genes, width)), name='likelihoo...]
where the time goes in v4:
time: 37.3 us; the launch traced here: 37.1 us
  Pallas kernels  36.5 us (98%)
  between operations  0.64 us (2%)
    pallas_call x1, Pallas kernels, likelihoods(): pl.pallas_call(functools.partial(kernel, (genes, width)), name='likelihoo...  35.2 us
    pallas_call x1, Pallas kernels, finish(): pl.pallas_call(functools.partial(finish_kernel, scale), name='finish', ou...  1.31 us

profile of v4, /device:TPU:1, one launch (start us, length us, event | category | flops | bytes accessed | tf_op | source)
XLA Modules:
  0.0 37.1 jit_solution(7641390852356134491)
XLA Ops:
  0.6 35.2 %likelihoods.1 = (f32[1,2048]{1,0:T(1,128)}, f32[1,128]{1,0:T(1,128)}, f32[1,128]{1,0:T(1,128)}) custom-call(s32[2,31]{1,0:T(2,128)} %bitcast.4, s32[1,16]{1,0:T(1,128)} %gene_ref.1, s32[1,16]{1,0:T(1,128)} %count_ref.1, f32[20]{0:T(128)} %freqs_ref.1, f32[4]{0:T(128)} %rates_ref.1, f32[62]{0:T(128)} %branch_ref.1, f32[20,20]{1,0:T(8,128)} %exchange_ref.1, ...), custom_call_target="tpu_custom_call" | custom-call | tf_op jit(solution)/shard_map/likelihoods/pallas_call | solution.py:374
  35.8 1.3 %finish.1 = (f32[1,2048]{1,0:T(1,128)}, f32[1,64]{1,0:T(1,128)}, f32[1,1]{1,0:T(1,128)}) custom-call(f32[1,2048]{1,0:T(1,128)} %get-tuple-element.9.values_ref, f32[1,128]{1,0:T(1,128)} %get-tuple-element.10.sums_ref, f32[1,128]{1,0:T(1,128)} %get-tuple-element.11.total_ref), custom_call_target="tpu_custom_call" | custom-call | tf_op jit(solution)/shard_map/finish/pallas_call | solution.py:428

commit v5 on v4

--- a/solution.py
+++ b/solution.py
@@ -46,10 +46,11 @@
     total = jnp.sum(pi_sub, axis=0, keepdims=True)
     pi_sub = pi_sub / total
     pi_lane = pi_lane / total
-    off = jnp.where(sub == lane, 0.0, both * 0.5 * pi_sub)
-    out_rate = jnp.sum(off, axis=0, keepdims=True)
+    sym = jnp.where(sub == lane, 0.0, both * 0.5)
+    out_rate = jnp.sum(sym * pi_sub, axis=0, keepdims=True)
     mean_rate = jnp.sum(out_rate * pi_lane[0:1], axis=1, keepdims=True)
-    gen = (off - jnp.where(sub == lane, out_rate, 0.0)) / mean_rate
+    root_sub, root_lane = jnp.sqrt(pi_sub), jnp.sqrt(pi_lane)
+    gen = (sym * root_sub * root_lane - jnp.where(sub == lane, out_rate, 0.0)) / mean_rate
 
     def times(left, right):
         acc = left[:, 0:1] * right[0:1, :]
@@ -91,26 +92,40 @@
             acc = columns[7]
             for order in range(6, -1, -1):
                 acc = columns[order] + acc * taus[half]
-            mat_ref[0, half, i * PAD : (i + 1) * PAD, :] = eye + acc * taus[half]
-
-
-def square(step, half, mat_ref, beside=None):
+            mat_ref[0, half, i * FLAT : i * FLAT + PAD, :] = eye + acc * taus[half]
+
+
+def rows_of(src, half, mid, group, mat_ref):
+    if group >= mid // 8:
+        return mat_ref[src, half, pl.ds(mid * FLAT + 8 * group, 8), :]
+    return mat_ref[src, half, pl.ds(8 * group * FLAT + mid, 8, stride=FLAT), :]
+
+
+def square(step, half, mat_ref, whole, beside=None):
     src = lax.rem(step, 2)
     dst = 1 - src
     for first in range(0, STATES, 4):
         if beside is not None:
             beside(first // 4)
-        accs = [None] * 4
+        groups = range(0 if whole is not None else first // 8, PAD // 8)
+        accs = {}
         for mid in range(STATES):
-            row = mat_ref[src, half, mid * PAD : (mid + 1) * PAD, :]
-            for at in range(4):
-                where = (first + at) * PAD + mid
-                factor = mat_ref[src, half, where : where + 1, :]
-                term = factor * row
-                accs[at] = term if accs[at] is None else accs[at] + term
-        for at in range(4):
-            start = (first + at) * PAD
-            mat_ref[dst, half, start : start + PAD, :] = accs[at]
+            rows = {group: rows_of(src, half, mid, group, mat_ref) for group in groups}
+            for i in range(first, first + 4):
+                low, high = (i, mid) if mid // 8 >= i // 8 else (mid, i)
+                factor = mat_ref[src, half, pl.ds(low * FLAT + high, 1), :]
+                for group in groups:
+                    term = factor * rows[group]
+                    accs[i, group] = term if mid == 0 else accs[i, group] + term
+        for i in range(first, first + 4):
+            for group in groups:
+                value = accs[i, group]
+                start = i * FLAT + 8 * group
+                if whole is not None:
+                    root = whole[8 * group : 8 * group + 8]
+                    value = value * (root / whole[i : i + 1])
+                    start = i * PAD + 8 * group
+                mat_ref[dst, half, pl.ds(start, 8), :] = value
 
 
 def tree_order(children_ref, order_ref):
@@ -318,28 +333,37 @@
     taylor(powers, rates_ref, branch_ref, mat_ref)
     per_step = chunks // SQUARINGS
 
-    def leaf_branches(step, carry):
+    def gather(step):
         for at in range(per_step):
             chunk = step * per_step + at
             fetch(chunk).wait()
             gather_leaves(chunk, tips_ref, order_ref, flat_ref, leaves_ref)
-        square(step, 0, mat_ref)
+
+    def leaf_branches(step, carry):
+        gather(step)
+        square(step, 0, mat_ref, None)
         return carry
 
-    lax.fori_loop(0, SQUARINGS, leaf_branches, 0)
+    lax.fori_loop(0, SQUARINGS - 1, leaf_branches, 0)
+    gather(SQUARINGS - 1)
+    square(SQUARINGS - 1, 0, mat_ref, jnp.sqrt(pi_sub))
     spread(0, mat_ref, spread_ref)
     leaf_operands(order_ref, spread_ref, leaf_ref)
 
-    def inner_branches(step, carry):
+    def inner_branches(step, whole):
         def beside(number):
             for at in range(per_step):
                 nodes = range(LEAVES // 2 * number // 5, LEAVES // 2 * (number + 1) // 5)
                 prune_leaves(nodes, step * per_step + at, leaves_ref, leaf_ref, level_refs[0])
 
-        square(step, 1, mat_ref, beside)
+        square(step, 1, mat_ref, whole, beside)
+
+    def triangles(step, carry):
+        inner_branches(step, None)
         return carry
 
-    lax.fori_loop(0, SQUARINGS, inner_branches, 0)
+    lax.fori_loop(0, SQUARINGS - 1, triangles, 0)
+    inner_branches(SQUARINGS - 1, jnp.sqrt(pi_sub))
     spread(1, mat_ref, spread_ref)
     inner_operands(order_ref, spread_ref, inner_ref)
     results = prune_inner(chunks, inner_ref, level_refs, weight_ref[:, 0:1])

time: 37.3 us -> 35.4 us (0.949)
  Pallas kernels: 36.5 us -> 34.5 us
    pallas_call x1, Pallas kernels: 35.2 us -> 33.2 us  [likelihoods(): pl.pallas_call(functools.partial(kernel, (genes, width)), name='likelihoo...]
where the time goes in v5:
time: 35.4 us; the launch traced here: 35.2 us
  Pallas kernels  34.5 us (97%)
  between operations  0.64 us (2%)
    pallas_call x1, Pallas kernels, likelihoods(): pl.pallas_call(functools.partial(kernel, (genes, width)), name='likelihoo...  33.2 us
    pallas_call x1, Pallas kernels, finish(): pl.pallas_call(functools.partial(finish_kernel, scale), name='finish', ou...  1.31 us

profile of v5, /device:TPU:1, one launch (start us, length us, event | category | flops | bytes accessed | tf_op | source)
XLA Modules:
  0.0 35.2 jit_solution(14706121036468551634)
XLA Ops:
  0.6 33.2 %likelihoods.1 = (f32[1,2048]{1,0:T(1,128)}, f32[1,128]{1,0:T(1,128)}, f32[1,128]{1,0:T(1,128)}) custom-call(s32[2,31]{1,0:T(2,128)} %bitcast.4, s32[1,16]{1,0:T(1,128)} %gene_ref.1, s32[1,16]{1,0:T(1,128)} %count_ref.1, f32[20]{0:T(128)} %freqs_ref.1, f32[4]{0:T(128)} %rates_ref.1, f32[62]{0:T(128)} %branch_ref.1, f32[20,20]{1,0:T(8,128)} %exchange_ref.1, ...), custom_call_target="tpu_custom_call" | custom-call | tf_op jit(solution)/shard_map/likelihoods/pallas_call | solution.py:398
  33.9 1.3 %finish.1 = (f32[1,2048]{1,0:T(1,128)}, f32[1,64]{1,0:T(1,128)}, f32[1,1]{1,0:T(1,128)}) custom-call(f32[1,2048]{1,0:T(1,128)} %get-tuple-element.9.values_ref, f32[1,128]{1,0:T(1,128)} %get-tuple-element.10.sums_ref, f32[1,128]{1,0:T(1,128)} %get-tuple-element.11.total_ref), custom_call_target="tpu_custom_call" | custom-call | tf_op jit(solution)/shard_map/finish/pallas_call | solution.py:452

commit v6 on v5

--- a/solution.py
+++ b/solution.py
@@ -84,15 +84,19 @@
         for at in range(min(SPLIT, NODES - half * SPLIT)):
             length = jnp.where(lane % SPLIT == at, branch_ref[half * SPLIT + at], length)
         taus.append(length * rate / 256.0)
-    sub = iota((PAD, LANES), 0)
     for i in range(STATES):
-        columns = [jnp.broadcast_to(p[:, i : i + 1], (PAD, LANES)) for p in powers]
-        eye = jnp.where(sub == i, 1.0, 0.0)
+        skip = i // 8 * 8
+        shape = (PAD - skip, LANES)
+        columns = [jnp.broadcast_to(p[skip:, i : i + 1], shape) for p in powers]
+        eye = jnp.where(iota(shape, 0) == i - skip, 1.0, 0.0)
         for half in range(2):
             acc = columns[7]
             for order in range(6, -1, -1):
                 acc = columns[order] + acc * taus[half]
-            mat_ref[0, half, i * FLAT : i * FLAT + PAD, :] = eye + acc * taus[half]
+            acc = eye + acc * taus[half]
+            for row in range(0, PAD - skip, 8):
+                start = i * FLAT + skip + row
+                mat_ref[0, half, pl.ds(start, 8), :] = acc[row : row + 8]
 
 
 def rows_of(src, half, mid, group, mat_ref):
@@ -122,8 +126,8 @@
                 value = accs[i, group]
                 start = i * FLAT + 8 * group
                 if whole is not None:
-                    root = whole[8 * group : 8 * group + 8]
-                    value = value * (root / whole[i : i + 1])
+                    root, inverse = whole
+                    value = value * root[8 * group : 8 * group + 8] * inverse[i : i + 1]
                     start = i * PAD + 8 * group
                 mat_ref[dst, half, pl.ds(start, 8), :] = value
 
@@ -308,10 +312,6 @@
 ):
     genes, sites = mesh_shape
     barrier = pltpu.get_barrier_semaphore()
-    for axis, size in (("site", sites), ("gene", genes)):
-        for off in range(1, size):
-            peer = lax.rem(lax.axis_index(axis) + off, size)
-            pl.semaphore_signal(barrier, inc=1, device_id={axis: peer})
     chunks = site_ref.shape[1] // CHUNK
 
     def fetch(chunk):
@@ -333,6 +333,9 @@
     taylor(powers, rates_ref, branch_ref, mat_ref)
     per_step = chunks // SQUARINGS
 
+    root = jnp.sqrt(pi_sub)
+    whole = (root, 1.0 / root)
+
     def gather(step):
         for at in range(per_step):
             chunk = step * per_step + at
@@ -345,8 +348,12 @@
         return carry
 
     lax.fori_loop(0, SQUARINGS - 1, leaf_branches, 0)
+    for axis, size in (("site", sites), ("gene", genes)):
+        for off in range(1, size):
+            peer = lax.rem(lax.axis_index(axis) + off, size)
+            pl.semaphore_signal(barrier, inc=1, device_id={axis: peer})
     gather(SQUARINGS - 1)
-    square(SQUARINGS - 1, 0, mat_ref, jnp.sqrt(pi_sub))
+    square(SQUARINGS - 1, 0, mat_ref, whole)
     spread(0, mat_ref, spread_ref)
     leaf_operands(order_ref, spread_ref, leaf_ref)
 
@@ -363,7 +370,7 @@
         return carry
 
     lax.fori_loop(0, SQUARINGS - 1, triangles, 0)
-    inner_branches(SQUARINGS - 1, jnp.sqrt(pi_sub))
+    inner_branches(SQUARINGS - 1, whole)
     spread(1, mat_ref, spread_ref)
     inner_operands(order_ref, spread_ref, inner_ref)
     results = prune_inner(chunks, inner_ref, level_refs, weight_ref[:, 0:1])

time: 35.4 us -> 35.4 us (level)
  no operation moved by 1% of the time
where the time goes in v6:
time: 35.4 us; the launch traced here: 35.2 us
  Pallas kernels  34.5 us (97%)
  between operations  0.64 us (2%)
    pallas_call x1, Pallas kernels, likelihoods(): pl.pallas_call(functools.partial(kernel, (genes, width)), name='likelihoo...  33.2 us
    pallas_call x1, Pallas kernels, finish(): pl.pallas_call(functools.partial(finish_kernel, scale), name='finish', ou...  1.31 us

profile of v6, /device:TPU:1, one launch (start us, length us, event | category | flops | bytes accessed | tf_op | source)
XLA Modules:
  0.0 35.2 jit_solution(15638790625288961219)
XLA Ops:
  0.6 33.2 %likelihoods.1 = (f32[1,2048]{1,0:T(1,128)}, f32[1,128]{1,0:T(1,128)}, f32[1,128]{1,0:T(1,128)}) custom-call(s32[2,31]{1,0:T(2,128)} %bitcast.4, s32[1,16]{1,0:T(1,128)} %gene_ref.1, s32[1,16]{1,0:T(1,128)} %count_ref.1, f32[20]{0:T(128)} %freqs_ref.1, f32[4]{0:T(128)} %rates_ref.1, f32[62]{0:T(128)} %branch_ref.1, f32[20,20]{1,0:T(8,128)} %exchange_ref.1, ...), custom_call_target="tpu_custom_call" | custom-call | tf_op jit(solution)/shard_map/likelihoods/pallas_call | solution.py:405
  33.9 1.3 %finish.1 = (f32[1,2048]{1,0:T(1,128)}, f32[1,64]{1,0:T(1,128)}, f32[1,1]{1,0:T(1,128)}) custom-call(f32[1,2048]{1,0:T(1,128)} %get-tuple-element.9.values_ref, f32[1,128]{1,0:T(1,128)} %get-tuple-element.10.sums_ref, f32[1,128]{1,0:T(1,128)} %get-tuple-element.11.total_ref), custom_call_target="tpu_custom_call" | custom-call | tf_op jit(solution)/shard_map/finish/pallas_call | solution.py:459
